TPU v7x, 32 devices: a whole 2x2x4 slice. The times are simulated.
32 devices in a mesh: dp: 4 (over x, core), pipe: 2 (over y), tensor: 4 (over z).
Axes of the slice: x: 2, y: 2, z: 4, core: 2. Of those that a mesh axis runs over, the one named last changes fastest.
Arguments:
- weights: bfloat16 [2816, 1408], P(('dp', 'pipe', 'tensor')), may hold values from -6 to 6
- first_moment: bfloat16 [2816, 1408], P(('dp', 'pipe', 'tensor')), may hold values from -6 to 6
- second_moment: bfloat16 [2816, 1408], P(('dp', 'pipe', 'tensor')), may hold values from 0.049804688 to 5
- row_weight: float32 [1408], replicated, may hold values from -1 to 1
- col_weight: float32 [1408], replicated, may hold values from 1 to 4
Outputs:
- weight_tiles: bfloat16 [2816, 1408], P(('pipe', 'tensor'))
- first_tiles: bfloat16 [2816, 1408], P(('pipe', 'tensor'))
- second_tiles: bfloat16 [2816, 1408], P(('pipe', 'tensor'))
- checksums: float32 [3, 2, 4, 11], P(None, 'pipe', 'tensor')
All inputs are finite; a program needn't handle non-finite values.
Results may differ from a plain program's by a relative error of at most 0.001.
Values may be sent and summed in bfloat16 or wider, within the bound.
A program may use at most 64 MiB of HBM per device.

v0:
```python
import jax
import jax.numpy as jnp
from jax import lax
from jax.sharding import PartitionSpec as P

CHECK_COLS = 128


def for_sending(array):
    return jax.tree.map(lambda a: a.astype(jnp.bfloat16) if a.dtype == jnp.float32 else a, array)


def column_sums(data, row_part, col_weight, col_blocks):
    row_mixed = jnp.dot(
        row_part[None, :], data.astype(jnp.float32), precision=lax.Precision.HIGHEST
    )[0]
    return jnp.sum((row_mixed * col_weight).reshape(col_blocks, -1), axis=1)


def shards(weights, first_moment, second_moment, row_weight, col_weight):
    dp_count = lax.axis_size("dp")
    pipe_count = lax.axis_size("pipe")
    tensor_count = lax.axis_size("tensor")
    shard_rows, width = weights.shape
    dp_section = dp_count // pipe_count
    tile_shards = dp_count // tensor_count
    piece_cols = width // dp_count
    tile_rows = shard_rows * dp_count
    col_blocks = width // CHECK_COLS
    factor = float(tile_rows * CHECK_COLS) ** (-0.5)
    sources = (weights, first_moment, second_moment)
    exchanged = (
        lax.all_to_all(sources[0], "dp", split_axis=1, concat_axis=0, tiled=True),
        lax.all_to_all(sources[1], "dp", split_axis=1, concat_axis=0, tiled=True),
        lax.all_to_all(sources[2], "dp", split_axis=1, concat_axis=0, tiled=True),
    )
    grouped = tuple(
        (item.reshape(pipe_count, dp_section, shard_rows, piece_cols) for item in exchanged)
    )
    sectioned = jax.tree.map(
        lambda part, own: part.astype(own.dtype),
        lax.all_to_all(for_sending(grouped), "pipe", split_axis=0, concat_axis=2, tiled=True),
        grouped,
    )
    routed = tuple(
        (item.reshape(tensor_count, tile_shards, 1, shard_rows, piece_cols) for item in sectioned)
    )
    arrived = jax.tree.map(
        lambda part, own: part.astype(own.dtype),
        lax.all_to_all(for_sending(routed), "tensor", split_axis=0, concat_axis=2, tiled=True),
        routed,
    )
    flat_pieces = tuple((item.reshape(tile_rows, piece_cols) for item in arrived))
    tiles = jax.tree.map(
        lambda part, own: part.astype(own.dtype),
        lax.all_gather(for_sending(flat_pieces), "dp", axis=1, tiled=True),
        flat_pieces,
    )
    tensor_pos = lax.axis_index("tensor")
    flat_index = (
        lax.axis_index("dp") * pipe_count + lax.axis_index("pipe")
    ) * tensor_count + tensor_pos
    in_section = flat_index % (dp_count * tensor_count)
    section_of = flat_index // (dp_count * tensor_count)
    tile_of = in_section // dp_count
    row_part = lax.dynamic_slice_in_dim(row_weight, in_section * shard_rows, shard_rows)
    partial_value = jnp.stack(
        [column_sums(item, row_part, col_weight, col_blocks) for item in sources]
    )
    section_hit = (jnp.arange(pipe_count) == section_of).astype(jnp.float32)
    tile_hit = (jnp.arange(tensor_count) == tile_of).astype(jnp.float32)
    spread = (
        partial_value[:, None, None, :]
        * section_hit[None, :, None, None]
        * tile_hit[None, None, :, None]
    )
    summed = lax.psum(spread, ("dp", "pipe", "tensor"))
    checks = (
        lax.dynamic_slice(summed, (0, lax.axis_index("pipe"), tensor_pos, 0), (3, 1, 1, col_blocks))
        * factor
    )
    return (tiles[0], tiles[1], tiles[2], checks)


def solution(mesh):
    return jax.shard_map(
        shards,
        mesh=mesh,
        in_specs=(
            P(("dp", "pipe", "tensor"), None),
            P(("dp", "pipe", "tensor"), None),
            P(("dp", "pipe", "tensor"), None),
            P(),
            P(),
        ),
        out_specs=(
            P(("pipe", "tensor"), None),
            P(("pipe", "tensor"), None),
            P(("pipe", "tensor"), None),
            P(None, "pipe", "tensor", None),
        ),
        check_vma=False,
    )
```

profile of v0, /device:TPU:0, one launch (start us, length us, event | category | flops | bytes accessed | tf_op | source)
XLA Modules:
  0.0 154.1 jit_solution(8427268718347811385)
XLA Ops:
  0.6 0.0 copy-start
  0.6 0.0 copy-start.3
  0.7 1.3 all_to_all.90
  1.9 0.7 copy.33
  2.7 0.0 copy-start.2
  2.7 4.4 %all-to-all-start = ((bf16[88,4,352]{2,0,1:T(8,128)(2,1)}), bf16[88,4,352]{2,0,1:T(8,128)(2,1)}, u32[]{:S(2)}, u32[]{:S(2)}) async-start(bf16[88,4,352]{2,0,1:T(8,128)(2,1)} %copy.33), calls=%async_computation | async-start | bytes 540672 | tf_op jit(solution)/shard_map/all_to_all | solution.py:33
  7.0 0.0 copy-done.3
  7.0 0.3 all_to_all.97
  7.3 0.7 copy.37
  8.1 0.0 copy-start.1
  8.1 5.6 %all-to-all-done = bf16[88,4,352]{2,0,1:T(8,128)(2,1)} async-done(((bf16[88,4,352]{2,0,1:T(8,128)(2,1)}), bf16[88,4,352]{2,0,1:T(8,128)(2,1)}, u32[]{:S(2)}, u32[]{:S(2)}) %all-to-all-start) | async-done | bytes 247840 | tf_op jit(solution)/shard_map/all_to_all | solution.py:33
  13.7 4.1 %all-to-all-start.3 = ((bf16[88,4,352]{2,0,1:T(8,128)(2,1)}), bf16[88,4,352]{2,0,1:T(8,128)(2,1)}, u32[]{:S(2)}, u32[]{:S(2)}) async-start(bf16[88,4,352]{2,0,1:T(8,128)(2,1)} %copy.37), calls=%async_computation.3 | async-start | bytes 540672 | tf_op jit(solution)/shard_map/all_to_all | solution.py:34
  17.8 0.0 copy-done.2
  17.8 0.3 all_to_all.104
  18.1 0.0 copy-start.4
  18.1 0.7 copy.41
  18.9 5.1 %all-to-all-done.3 = bf16[88,4,352]{2,0,1:T(8,128)(2,1)} async-done(((bf16[88,4,352]{2,0,1:T(8,128)(2,1)}), bf16[88,4,352]{2,0,1:T(8,128)(2,1)}, u32[]{:S(2)}, u32[]{:S(2)}) %all-to-all-start.3) | async-done | bytes 247840 | tf_op jit(solution)/shard_map/all_to_all | solution.py:34
  24.0 4.1 %all-to-all-start.6 = ((bf16[88,4,352]{2,0,1:T(8,128)(2,1)}), bf16[88,4,352]{2,0,1:T(8,128)(2,1)}, u32[]{:S(2)}, u32[]{:S(2)}) async-start(bf16[88,4,352]{2,0,1:T(8,128)(2,1)} %copy.41), calls=%async_computation.6 | async-start | bytes 540672 | tf_op jit(solution)/shard_map/all_to_all | solution.py:35
  28.0 0.0 copy-done
  28.1 0.0 copy-done.1
  28.1 0.3 convolution_reduce_fusion.2
  28.4 0.3 convolution_reduce_fusion
  28.7 5.5 %all-to-all-done.6 = bf16[88,4,352]{2,0,1:T(8,128)(2,1)} async-done(((bf16[88,4,352]{2,0,1:T(8,128)(2,1)}), bf16[88,4,352]{2,0,1:T(8,128)(2,1)}, u32[]{:S(2)}, u32[]{:S(2)}) %all-to-all-start.6) | async-done | bytes 247840 | tf_op jit(solution)/shard_map/all_to_all | solution.py:35
  34.2 3.6 %all-to-all-start.1 = ((bf16[2,2,88,352]{3,2,1,0:T(8,128)(2,1)}), bf16[2,2,88,352]{3,2,1,0:T(8,128)(2,1)S(1)}, u32[]{:S(2)}, u32[]{:S(2)}) async-start(bf16[2,2,88,352]{3,2,1,0:T(8,128)(2,1)} %bitcast.1), calls=%async_computation.1 | async-start | bytes 540672 | tf_op jit(solution)/shard_map/all_to_all | solution.py:42
  37.8 0.3 convolution_reduce_fusion.1
  38.1 0.0 copy-done.4
  38.1 0.1 bitcast_reduce_fusion.2
  38.3 5.2 %all-to-all-done.1 = bf16[2,2,88,352]{3,2,1,0:T(8,128)(2,1)S(1)} async-done(((bf16[2,2,88,352]{3,2,1,0:T(8,128)(2,1)}), bf16[2,2,88,352]{3,2,1,0:T(8,128)(2,1)S(1)}, u32[]{:S(2)}, u32[]{:S(2)}) %all-to-all-start.1) | async-done | bytes 247840 | tf_op jit(solution)/shard_map/all_to_all | solution.py:42
  43.5 3.4 %all-to-all-start.4 = ((bf16[2,2,88,352]{3,2,1,0:T(8,128)(2,1)}), bf16[2,2,88,352]{3,2,1,0:T(8,128)(2,1)S(1)}, u32[]{:S(2)}, u32[]{:S(2)}) async-start(bf16[2,2,88,352]{3,2,1,0:T(8,128)(2,1)} %bitcast.8), calls=%async_computation.4 | async-start | bytes 540672 | tf_op jit(solution)/shard_map/all_to_all | solution.py:42
  47.0 5.2 %all-to-all-done.4 = bf16[2,2,88,352]{3,2,1,0:T(8,128)(2,1)S(1)} async-done(((bf16[2,2,88,352]{3,2,1,0:T(8,128)(2,1)}), bf16[2,2,88,352]{3,2,1,0:T(8,128)(2,1)S(1)}, u32[]{:S(2)}, u32[]{:S(2)}) %all-to-all-start.4) | async-done | bytes 247840 | tf_op jit(solution)/shard_map/all_to_all | solution.py:42
  52.1 3.4 %all-to-all-start.7 = ((bf16[2,2,88,352]{3,2,1,0:T(8,128)(2,1)}), bf16[2,2,88,352]{3,2,1,0:T(8,128)(2,1)S(1)}, u32[]{:S(2)}, u32[]{:S(2)}) async-start(bf16[2,2,88,352]{3,2,1,0:T(8,128)(2,1)} %bitcast.15), calls=%async_computation.7 | async-start | bytes 540672 | tf_op jit(solution)/shard_map/all_to_all | solution.py:42
  55.6 0.1 broadcast_multiply_fusion.1
  55.6 0.7 copy.34
  56.4 4.4 %all-to-all-done.7 = bf16[2,2,88,352]{3,2,1,0:T(8,128)(2,1)S(1)} async-done(((bf16[2,2,88,352]{3,2,1,0:T(8,128)(2,1)}), bf16[2,2,88,352]{3,2,1,0:T(8,128)(2,1)S(1)}, u32[]{:S(2)}, u32[]{:S(2)}) %all-to-all-start.7) | async-done | bytes 247840 | tf_op jit(solution)/shard_map/all_to_all | solution.py:42
  60.8 5.1 %all-to-all-start.2 = ((bf16[4,1,1,88,352]{4,3,2,1,0:T(8,128)(2,1)}), bf16[4,1,1,88,352]{4,3,2,1,0:T(8,128)(2,1)S(1)}, u32[]{:S(2)}, u32[]{:S(2)}) async-start(bf16[4,1,1,88,352]{4,3,2,1,0:T(8,128)(2,1)} %bitcast.5), calls=%async_computation.2 | async-start | bytes 540672 | tf_op jit(solution)/shard_map/all_to_all | solution.py:50
  65.9 0.1 broadcast_multiply_fusion
  65.9 39.9 %psum.7 = f32[3,2,4,11]{3,2,1,0:T(4,128)S(1)} all-reduce(f32[3,2,4,11]{3,2,1,0:T(4,128)S(1)} %broadcast_multiply_fusion), channel_id=1, replica_groups=mesh['dp'=4,'pipe'=2,'tensor'=4] {'dp','pipe','tensor'}, use_global_device_ids=true, to_apply=%region_3.4 | all-reduce | flops 264 | bytes 2112 | tf_op jit(solution)/shard_map/psum | solution.py:77
  105.8 0.6 dynamic-slice_multiply_fusion
  106.4 0.7 copy.38
  107.1 0.7 copy.42
  107.9 0.0 all-to-all-done.2
  107.9 3.6 %all-to-all-start.5 = ((bf16[4,1,1,88,352]{4,3,2,1,0:T(8,128)(2,1)}), bf16[4,1,1,88,352]{4,3,2,1,0:T(8,128)(2,1)S(1)}, u32[]{:S(2)}, u32[]{:S(2)}) async-start(bf16[4,1,1,88,352]{4,3,2,1,0:T(8,128)(2,1)} %bitcast.12), calls=%async_computation.5 | async-start | bytes 540672 | tf_op jit(solution)/shard_map/all_to_all | solution.py:50
  111.4 0.2 copy.36
  111.6 11.0 %all_gather.9 = bf16[352,1408]{0,1:T(8,128)(2,1)S(1)} all-gather(bf16[352,352]{0,1:T(8,128)(2,1)S(1)} %copy.36), channel_id=1, replica_groups=mesh['dp'=4,'pipe'=2,'tensor'=4] {'dp'}, dimensions={1}, use_global_device_ids=true | all-gather | bytes 1239040 | tf_op jit(solution)/shard_map/all_gather | solution.py:56
  122.6 1.9 %copy.45 = bf16[352,1408]{1,0:T(8,128)(2,1)} copy(bf16[352,1408]{0,1:T(8,128)(2,1)S(1)} %all_gather.9) | data formatting | bytes 1982464
  124.5 0.0 all-to-all-done.5
  124.5 5.1 %all-to-all-start.8 = ((bf16[4,1,1,88,352]{4,3,2,1,0:T(8,128)(2,1)}), bf16[4,1,1,88,352]{4,3,2,1,0:T(8,128)(2,1)S(1)}, u32[]{:S(2)}, u32[]{:S(2)}) async-start(bf16[4,1,1,88,352]{4,3,2,1,0:T(8,128)(2,1)} %bitcast.19), calls=%async_computation.8 | async-start | bytes 540672 | tf_op jit(solution)/shard_map/all_to_all | solution.py:50
  129.6 0.2 copy.40
  129.8 10.0 %all_gather.10 = bf16[352,1408]{0,1:T(8,128)(2,1)S(1)} all-gather(bf16[352,352]{0,1:T(8,128)(2,1)S(1)} %copy.40), channel_id=1, replica_groups=mesh['dp'=4,'pipe'=2,'tensor'=4] {'dp'}, dimensions={1}, use_global_device_ids=true | all-gather | bytes 1239040 | tf_op jit(solution)/shard_map/all_gather | solution.py:56
  139.8 1.9 %copy.46 = bf16[352,1408]{1,0:T(8,128)(2,1)} copy(bf16[352,1408]{0,1:T(8,128)(2,1)S(1)} %all_gather.10) | data formatting | bytes 1982464
  141.7 0.0 all-to-all-done.8
  141.7 0.2 copy.44
  141.9 10.3 %all_gather.11 = bf16[352,1408]{0,1:T(8,128)(2,1)S(1)} all-gather(bf16[352,352]{0,1:T(8,128)(2,1)S(1)} %copy.44), channel_id=1, replica_groups=mesh['dp'=4,'pipe'=2,'tensor'=4] {'dp'}, dimensions={1}, use_global_device_ids=true | all-gather | bytes 1239040 | tf_op jit(solution)/shard_map/all_gather | solution.py:56
  152.2 1.9 %copy.47 = bf16[352,1408]{1,0:T(8,128)(2,1)} copy(bf16[352,1408]{0,1:T(8,128)(2,1)S(1)} %all_gather.11) | data formatting | bytes 1982464
  (3 shorter events, 0.0 us)
Async XLA Ops:
  0.6 27.4 %copy-start = (f32[1408]{0:T(1024)S(1)}, f32[1408]{0:T(1024)}, u32[]{:S(2)}) copy-start(f32[1408]{0:T(1024)} %param.8) | copy-start | bytes 16900
  0.6 6.4 %copy-start.3 = (bf16[88,1408]{1,0:T(8,128)(2,1)S(1)}, bf16[88,1408]{1,0:T(8,128)(2,1)}, u32[]{:S(2)}) copy-start(bf16[88,1408]{1,0:T(8,128)(2,1)} %param.6) | copy-start | bytes 743428
  2.7 15.2 %copy-start.2 = (bf16[88,1408]{1,0:T(8,128)(2,1)S(1)}, bf16[88,1408]{1,0:T(8,128)(2,1)}, u32[]{:S(2)}) copy-start(bf16[88,1408]{1,0:T(8,128)(2,1)} %param.7) | copy-start | bytes 743428
  2.7 11.0 %all-to-all-start = ((bf16[88,4,352]{2,0,1:T(8,128)(2,1)}), bf16[88,4,352]{2,0,1:T(8,128)(2,1)}, u32[]{:S(2)}, u32[]{:S(2)}) async-start(bf16[88,4,352]{2,0,1:T(8,128)(2,1)} %copy.33), calls=%async_computation | async-start | bytes 540672 | tf_op jit(solution)/shard_map/all_to_all | solution.py:33
  8.1 20.0 %copy-start.1 = (bf16[88,1408]{1,0:T(8,128)(2,1)S(1)}, bf16[88,1408]{1,0:T(8,128)(2,1)}, u32[]{:S(2)}) copy-start(bf16[88,1408]{1,0:T(8,128)(2,1)} %param.5) | copy-start | bytes 743428
  13.7 10.2 %all-to-all-start.3 = ((bf16[88,4,352]{2,0,1:T(8,128)(2,1)}), bf16[88,4,352]{2,0,1:T(8,128)(2,1)}, u32[]{:S(2)}, u32[]{:S(2)}) async-start(bf16[88,4,352]{2,0,1:T(8,128)(2,1)} %copy.37), calls=%async_computation.3 | async-start | bytes 540672 | tf_op jit(solution)/shard_map/all_to_all | solution.py:34
  18.1 20.0 %copy-start.4 = (f32[1408]{0:T(1024)S(1)}, f32[1408]{0:T(1024)}, u32[]{:S(2)}) copy-start(f32[1408]{0:T(1024)} %param.9) | copy-start | bytes 16900
  24.0 10.2 %all-to-all-start.6 = ((bf16[88,4,352]{2,0,1:T(8,128)(2,1)}), bf16[88,4,352]{2,0,1:T(8,128)(2,1)}, u32[]{:S(2)}, u32[]{:S(2)}) async-start(bf16[88,4,352]{2,0,1:T(8,128)(2,1)} %copy.41), calls=%async_computation.6 | async-start | bytes 540672 | tf_op jit(solution)/shard_map/all_to_all | solution.py:35
  34.2 9.3 %all-to-all-start.1 = ((bf16[2,2,88,352]{3,2,1,0:T(8,128)(2,1)}), bf16[2,2,88,352]{3,2,1,0:T(8,128)(2,1)S(1)}, u32[]{:S(2)}, u32[]{:S(2)}) async-start(bf16[2,2,88,352]{3,2,1,0:T(8,128)(2,1)} %bitcast.1), calls=%async_computation.1 | async-start | bytes 540672 | tf_op jit(solution)/shard_map/all_to_all | solution.py:42
  43.5 8.7 %all-to-all-start.4 = ((bf16[2,2,88,352]{3,2,1,0:T(8,128)(2,1)}), bf16[2,2,88,352]{3,2,1,0:T(8,128)(2,1)S(1)}, u32[]{:S(2)}, u32[]{:S(2)}) async-start(bf16[2,2,88,352]{3,2,1,0:T(8,128)(2,1)} %bitcast.8), calls=%async_computation.4 | async-start | bytes 540672 | tf_op jit(solution)/shard_map/all_to_all | solution.py:42
  52.1 8.7 %all-to-all-start.7 = ((bf16[2,2,88,352]{3,2,1,0:T(8,128)(2,1)}), bf16[2,2,88,352]{3,2,1,0:T(8,128)(2,1)S(1)}, u32[]{:S(2)}, u32[]{:S(2)}) async-start(bf16[2,2,88,352]{3,2,1,0:T(8,128)(2,1)} %bitcast.15), calls=%async_computation.7 | async-start | bytes 540672 | tf_op jit(solution)/shard_map/all_to_all | solution.py:42
  60.8 47.1 %all-to-all-start.2 = ((bf16[4,1,1,88,352]{4,3,2,1,0:T(8,128)(2,1)}), bf16[4,1,1,88,352]{4,3,2,1,0:T(8,128)(2,1)S(1)}, u32[]{:S(2)}, u32[]{:S(2)}) async-start(bf16[4,1,1,88,352]{4,3,2,1,0:T(8,128)(2,1)} %bitcast.5), calls=%async_computation.2 | async-start | bytes 540672 | tf_op jit(solution)/shard_map/all_to_all | solution.py:50
  107.9 16.6 %all-to-all-start.5 = ((bf16[4,1,1,88,352]{4,3,2,1,0:T(8,128)(2,1)}), bf16[4,1,1,88,352]{4,3,2,1,0:T(8,128)(2,1)S(1)}, u32[]{:S(2)}, u32[]{:S(2)}) async-start(bf16[4,1,1,88,352]{4,3,2,1,0:T(8,128)(2,1)} %bitcast.12), calls=%async_computation.5 | async-start | bytes 540672 | tf_op jit(solution)/shard_map/all_to_all | solution.py:50
  124.5 17.2 %all-to-all-start.8 = ((bf16[4,1,1,88,352]{4,3,2,1,0:T(8,128)(2,1)}), bf16[4,1,1,88,352]{4,3,2,1,0:T(8,128)(2,1)S(1)}, u32[]{:S(2)}, u32[]{:S(2)}) async-start(bf16[4,1,1,88,352]{4,3,2,1,0:T(8,128)(2,1)} %bitcast.19), calls=%async_computation.8 | async-start | bytes 540672 | tf_op jit(solution)/shard_map/all_to_all | solution.py:50
where the time goes:
time: 155 us; the launch traced here: 154 us
  blocking collectives  71.2 us (46%)
  starting transfers between devices  36.7 us (24%)
  waiting for transfers between devices  31 us (20%)
  local copies, waits for them, and re-layouts  12.5 us (8%)
    psum x1, blocking collectives, shards(): summed = lax.psum(spread, ('dp', 'pipe', 'tensor'))  39.9 us
    all_gather x3, blocking collectives, shards(): lax.all_gather(for_sending(flat_pieces), 'dp', axis=1, tiled=True)  31.3 us
    all_to_all x3, waiting for transfers between devices, shards(): lax.all_to_all(for_sending(grouped), 'pipe', split_axis=0, concat_axis=2,...  14.7 us
    all_to_all x3, starting transfers between devices, shards(): lax.all_to_all(for_sending(routed), 'tensor', split_axis=0, concat_axis=2...  13.7 us
    all_to_all x3, starting transfers between devices, shards(): lax.all_to_all(for_sending(grouped), 'pipe', split_axis=0, concat_axis=2,...  10.5 us
    unnamed x13, local copies, waits for them, and re-layouts  5.65 us
    all_to_all x1, waiting for transfers between devices, shards(): lax.all_to_all(sources[0], 'dp', split_axis=1, concat_axis=0, tiled=True)  5.65 us
    all_to_all x1, waiting for transfers between devices, shards(): lax.all_to_all(sources[2], 'dp', split_axis=1, concat_axis=0, tiled=True)  5.51 us
  transfers between devices with their start and end apart: 9, of which 6 were waited for; matrix products, arithmetic and copies ran while one was open for 6% of the time, Pallas kernels for 0%

commit v1 on v0

--- a/solution.py
+++ b/solution.py
@@ -74,7 +74,10 @@
         * section_hit[None, :, None, None]
         * tile_hit[None, None, :, None]
     )
-    summed = lax.psum(spread, ("dp", "pipe", "tensor"))
+    marks_render = lambda axis_tag, mesh_name, array_in: jax.lax.psum(
+        jax.lax.psum(array_in, mesh_name), axis_tag
+    )
+    summed = marks_render("dp", ("pipe", "tensor"), array_in=spread)
     checks = (
         lax.dynamic_slice(summed, (0, lax.axis_index("pipe"), tensor_pos, 0), (3, 1, 1, col_blocks))
         * factor

time: 155 us -> 160 us (1.032)
  blocking collectives: 71.2 us -> 76.4 us
    psum x1 -> x2, blocking collectives: 39.9 us -> 46.7 us  [the longest x1 36.3 us: shards(): jax.lax.psum(array_in, mesh_name)]
where the time goes in v1:
time: 160 us; the launch traced here: 159 us
  blocking collectives  76.4 us (48%)
  starting transfers between devices  36.6 us (23%)
  waiting for transfers between devices  31 us (19%)
  local copies, waits for them, and re-layouts  12.5 us (8%)
    psum x1, blocking collectives, shards(): jax.lax.psum(array_in, mesh_name)  36.3 us
    all_gather x3, blocking collectives, shards(): lax.all_gather(for_sending(flat_pieces), 'dp', axis=1, tiled=True)  29.8 us
    all_to_all x3, waiting for transfers between devices, shards(): lax.all_to_all(for_sending(grouped), 'pipe', split_axis=0, concat_axis=2,...  14.7 us
    all_to_all x3, starting transfers between devices, shards(): lax.all_to_all(for_sending(routed), 'tensor', split_axis=0, concat_axis=2...  13.6 us
    all_to_all x3, starting transfers between devices, shards(): lax.all_to_all(for_sending(grouped), 'pipe', split_axis=0, concat_axis=2,...  10.5 us
    psum x1, blocking collectives, shards(): jax.lax.psum(jax.lax.psum(array_in, mesh_name), axis_tag)  10.4 us
    all_to_all x1, waiting for transfers between devices, shards(): lax.all_to_all(sources[0], 'dp', split_axis=1, concat_axis=0, tiled=True)  5.65 us
    unnamed x13, local copies, waits for them, and re-layouts  5.65 us
  transfers between devices with their start and end apart: 9, of which 6 were waited for; matrix products, arithmetic and copies ran while one was open for 6% of the time, Pallas kernels for 0%

profile of v1, /device:TPU:0, one launch (start us, length us, event | category | flops | bytes accessed | tf_op | source)
XLA Modules:
  0.0 159.2 jit_solution(11384963092602040313)
XLA Ops:
  0.6 0.0 copy-start
  0.6 0.0 copy-start.3
  0.7 1.3 all_to_all.90
  1.9 0.7 copy.33
  2.7 0.0 copy-start.2
  2.7 4.4 %all-to-all-start = ((bf16[88,4,352]{2,0,1:T(8,128)(2,1)}), bf16[88,4,352]{2,0,1:T(8,128)(2,1)}, u32[]{:S(2)}, u32[]{:S(2)}) async-start(bf16[88,4,352]{2,0,1:T(8,128)(2,1)} %copy.33), calls=%async_computation | async-start | bytes 540672 | tf_op jit(solution)/shard_map/all_to_all | solution.py:33
  7.0 0.0 copy-done.3
  7.0 0.3 all_to_all.97
  7.3 0.7 copy.37
  8.1 0.0 copy-start.1
  8.1 5.7 %all-to-all-done = bf16[88,4,352]{2,0,1:T(8,128)(2,1)} async-done(((bf16[88,4,352]{2,0,1:T(8,128)(2,1)}), bf16[88,4,352]{2,0,1:T(8,128)(2,1)}, u32[]{:S(2)}, u32[]{:S(2)}) %all-to-all-start) | async-done | bytes 247840 | tf_op jit(solution)/shard_map/all_to_all | solution.py:33
  13.7 4.1 %all-to-all-start.3 = ((bf16[88,4,352]{2,0,1:T(8,128)(2,1)}), bf16[88,4,352]{2,0,1:T(8,128)(2,1)}, u32[]{:S(2)}, u32[]{:S(2)}) async-start(bf16[88,4,352]{2,0,1:T(8,128)(2,1)} %copy.37), calls=%async_computation.3 | async-start | bytes 540672 | tf_op jit(solution)/shard_map/all_to_all | solution.py:34
  17.8 0.0 copy-done.2
  17.9 0.3 all_to_all.104
  18.1 0.0 copy-start.4
  18.2 0.7 copy.41
  18.9 5.1 %all-to-all-done.3 = bf16[88,4,352]{2,0,1:T(8,128)(2,1)} async-done(((bf16[88,4,352]{2,0,1:T(8,128)(2,1)}), bf16[88,4,352]{2,0,1:T(8,128)(2,1)}, u32[]{:S(2)}, u32[]{:S(2)}) %all-to-all-start.3) | async-done | bytes 247840 | tf_op jit(solution)/shard_map/all_to_all | solution.py:34
  24.0 4.1 %all-to-all-start.6 = ((bf16[88,4,352]{2,0,1:T(8,128)(2,1)}), bf16[88,4,352]{2,0,1:T(8,128)(2,1)}, u32[]{:S(2)}, u32[]{:S(2)}) async-start(bf16[88,4,352]{2,0,1:T(8,128)(2,1)} %copy.41), calls=%async_computation.6 | async-start | bytes 540672 | tf_op jit(solution)/shard_map/all_to_all | solution.py:35
  28.1 0.0 copy-done
  28.1 0.0 copy-done.1
  28.1 0.3 convolution_reduce_fusion.2
  28.4 0.3 convolution_reduce_fusion
  28.7 5.5 %all-to-all-done.6 = bf16[88,4,352]{2,0,1:T(8,128)(2,1)} async-done(((bf16[88,4,352]{2,0,1:T(8,128)(2,1)}), bf16[88,4,352]{2,0,1:T(8,128)(2,1)}, u32[]{:S(2)}, u32[]{:S(2)}) %all-to-all-start.6) | async-done | bytes 247840 | tf_op jit(solution)/shard_map/all_to_all | solution.py:35
  34.2 3.6 %all-to-all-start.1 = ((bf16[2,2,88,352]{3,2,1,0:T(8,128)(2,1)}), bf16[2,2,88,352]{3,2,1,0:T(8,128)(2,1)S(1)}, u32[]{:S(2)}, u32[]{:S(2)}) async-start(bf16[2,2,88,352]{3,2,1,0:T(8,128)(2,1)} %bitcast.1), calls=%async_computation.1 | async-start | bytes 540672 | tf_op jit(solution)/shard_map/all_to_all | solution.py:42
  37.8 0.3 convolution_reduce_fusion.1
  38.1 0.0 copy-done.4
  38.1 0.1 bitcast_reduce_fusion.2
  38.3 5.2 %all-to-all-done.1 = bf16[2,2,88,352]{3,2,1,0:T(8,128)(2,1)S(1)} async-done(((bf16[2,2,88,352]{3,2,1,0:T(8,128)(2,1)}), bf16[2,2,88,352]{3,2,1,0:T(8,128)(2,1)S(1)}, u32[]{:S(2)}, u32[]{:S(2)}) %all-to-all-start.1) | async-done | bytes 247840 | tf_op jit(solution)/shard_map/all_to_all | solution.py:42
  43.5 3.4 %all-to-all-start.4 = ((bf16[2,2,88,352]{3,2,1,0:T(8,128)(2,1)}), bf16[2,2,88,352]{3,2,1,0:T(8,128)(2,1)S(1)}, u32[]{:S(2)}, u32[]{:S(2)}) async-start(bf16[2,2,88,352]{3,2,1,0:T(8,128)(2,1)} %bitcast.8), calls=%async_computation.4 | async-start | bytes 540672 | tf_op jit(solution)/shard_map/all_to_all | solution.py:42
  47.0 5.2 %all-to-all-done.4 = bf16[2,2,88,352]{3,2,1,0:T(8,128)(2,1)S(1)} async-done(((bf16[2,2,88,352]{3,2,1,0:T(8,128)(2,1)}), bf16[2,2,88,352]{3,2,1,0:T(8,128)(2,1)S(1)}, u32[]{:S(2)}, u32[]{:S(2)}) %all-to-all-start.4) | async-done | bytes 247840 | tf_op jit(solution)/shard_map/all_to_all | solution.py:42
  52.1 3.4 %all-to-all-start.7 = ((bf16[2,2,88,352]{3,2,1,0:T(8,128)(2,1)}), bf16[2,2,88,352]{3,2,1,0:T(8,128)(2,1)S(1)}, u32[]{:S(2)}, u32[]{:S(2)}) async-start(bf16[2,2,88,352]{3,2,1,0:T(8,128)(2,1)} %bitcast.15), calls=%async_computation.7 | async-start | bytes 540672 | tf_op jit(solution)/shard_map/all_to_all | solution.py:42
  55.6 0.1 broadcast_multiply_fusion.1
  55.7 0.7 copy.34
  56.4 4.4 %all-to-all-done.7 = bf16[2,2,88,352]{3,2,1,0:T(8,128)(2,1)S(1)} async-done(((bf16[2,2,88,352]{3,2,1,0:T(8,128)(2,1)}), bf16[2,2,88,352]{3,2,1,0:T(8,128)(2,1)S(1)}, u32[]{:S(2)}, u32[]{:S(2)}) %all-to-all-start.7) | async-done | bytes 247840 | tf_op jit(solution)/shard_map/all_to_all | solution.py:42
  60.8 5.1 %all-to-all-start.2 = ((bf16[4,1,1,88,352]{4,3,2,1,0:T(8,128)(2,1)}), bf16[4,1,1,88,352]{4,3,2,1,0:T(8,128)(2,1)S(1)}, u32[]{:S(2)}, u32[]{:S(2)}) async-start(bf16[4,1,1,88,352]{4,3,2,1,0:T(8,128)(2,1)} %bitcast.5), calls=%async_computation.2 | async-start | bytes 540672 | tf_op jit(solution)/shard_map/all_to_all | solution.py:50
  65.9 0.1 broadcast_multiply_fusion
  66.0 36.3 %psum.14 = f32[3,2,4,11]{3,2,1,0:T(4,128)S(1)} all-reduce(f32[3,2,4,11]{3,2,1,0:T(4,128)S(1)} %broadcast_multiply_fusion), channel_id=1, replica_groups=mesh['dp'=4,'pipe'=2,'tensor'=4] {'pipe','tensor'}, use_global_device_ids=true, to_apply=%region_3.4 | all-reduce | flops 264 | bytes 2112 | tf_op jit(solution)/shard_map/psum | solution.py:78
  102.2 10.4 %psum.15 = f32[3,2,4,11]{3,2,1,0:T(4,128)S(1)} all-reduce(f32[3,2,4,11]{3,2,1,0:T(4,128)S(1)} %psum.14), channel_id=1, replica_groups=mesh['dp'=4,'pipe'=2,'tensor'=4] {'dp'}, use_global_device_ids=true, to_apply=%region_4.5 | all-reduce | flops 264 | bytes 2112 | tf_op jit(solution)/shard_map/psum | solution.py:77
  112.6 0.6 dynamic-slice_multiply_fusion
  113.2 0.7 copy.38
  114.0 0.7 copy.42
  114.7 0.0 all-to-all-done.2
  114.7 3.5 %all-to-all-start.5 = ((bf16[4,1,1,88,352]{4,3,2,1,0:T(8,128)(2,1)}), bf16[4,1,1,88,352]{4,3,2,1,0:T(8,128)(2,1)S(1)}, u32[]{:S(2)}, u32[]{:S(2)}) async-start(bf16[4,1,1,88,352]{4,3,2,1,0:T(8,128)(2,1)} %bitcast.12), calls=%async_computation.5 | async-start | bytes 540672 | tf_op jit(solution)/shard_map/all_to_all | solution.py:50
  118.1 0.2 copy.36
  118.4 9.2 %all_gather.9 = bf16[352,1408]{0,1:T(8,128)(2,1)S(1)} all-gather(bf16[352,352]{0,1:T(8,128)(2,1)S(1)} %copy.36), channel_id=1, replica_groups=mesh['dp'=4,'pipe'=2,'tensor'=4] {'dp'}, dimensions={1}, use_global_device_ids=true | all-gather | bytes 1239040 | tf_op jit(solution)/shard_map/all_gather | solution.py:56
  127.6 1.9 %copy.45 = bf16[352,1408]{1,0:T(8,128)(2,1)} copy(bf16[352,1408]{0,1:T(8,128)(2,1)S(1)} %all_gather.9) | data formatting | bytes 1982464
  129.4 0.0 all-to-all-done.5
  129.4 5.1 %all-to-all-start.8 = ((bf16[4,1,1,88,352]{4,3,2,1,0:T(8,128)(2,1)}), bf16[4,1,1,88,352]{4,3,2,1,0:T(8,128)(2,1)S(1)}, u32[]{:S(2)}, u32[]{:S(2)}) async-start(bf16[4,1,1,88,352]{4,3,2,1,0:T(8,128)(2,1)} %bitcast.19), calls=%async_computation.8 | async-start | bytes 540672 | tf_op jit(solution)/shard_map/all_to_all | solution.py:50
  134.5 0.2 copy.40
  134.7 10.2 %all_gather.10 = bf16[352,1408]{0,1:T(8,128)(2,1)S(1)} all-gather(bf16[352,352]{0,1:T(8,128)(2,1)S(1)} %copy.40), channel_id=1, replica_groups=mesh['dp'=4,'pipe'=2,'tensor'=4] {'dp'}, dimensions={1}, use_global_device_ids=true | all-gather | bytes 1239040 | tf_op jit(solution)/shard_map/all_gather | solution.py:56
  144.9 1.9 %copy.46 = bf16[352,1408]{1,0:T(8,128)(2,1)} copy(bf16[352,1408]{0,1:T(8,128)(2,1)S(1)} %all_gather.10) | data formatting | bytes 1982464
  146.8 0.0 all-to-all-done.8
  146.8 0.2 copy.44
  147.0 10.3 %all_gather.11 = bf16[352,1408]{0,1:T(8,128)(2,1)S(1)} all-gather(bf16[352,352]{0,1:T(8,128)(2,1)S(1)} %copy.44), channel_id=1, replica_groups=mesh['dp'=4,'pipe'=2,'tensor'=4] {'dp'}, dimensions={1}, use_global_device_ids=true | all-gather | bytes 1239040 | tf_op jit(solution)/shard_map/all_gather | solution.py:56
  157.3 1.9 %copy.47 = bf16[352,1408]{1,0:T(8,128)(2,1)} copy(bf16[352,1408]{0,1:T(8,128)(2,1)S(1)} %all_gather.11) | data formatting | bytes 1982464
  (3 shorter events, 0.0 us)
Async XLA Ops:
  0.6 27.4 %copy-start = (f32[1408]{0:T(1024)S(1)}, f32[1408]{0:T(1024)}, u32[]{:S(2)}) copy-start(f32[1408]{0:T(1024)} %param.8) | copy-start | bytes 16900
  0.6 6.4 %copy-start.3 = (bf16[88,1408]{1,0:T(8,128)(2,1)S(1)}, bf16[88,1408]{1,0:T(8,128)(2,1)}, u32[]{:S(2)}) copy-start(bf16[88,1408]{1,0:T(8,128)(2,1)} %param.6) | copy-start | bytes 743428
  2.7 15.2 %copy-start.2 = (bf16[88,1408]{1,0:T(8,128)(2,1)S(1)}, bf16[88,1408]{1,0:T(8,128)(2,1)}, u32[]{:S(2)}) copy-start(bf16[88,1408]{1,0:T(8,128)(2,1)} %param.7) | copy-start | bytes 743428
  2.7 11.1 %all-to-all-start = ((bf16[88,4,352]{2,0,1:T(8,128)(2,1)}), bf16[88,4,352]{2,0,1:T(8,128)(2,1)}, u32[]{:S(2)}, u32[]{:S(2)}) async-start(bf16[88,4,352]{2,0,1:T(8,128)(2,1)} %copy.33), calls=%async_computation | async-start | bytes 540672 | tf_op jit(solution)/shard_map/all_to_all | solution.py:33
  8.1 20.0 %copy-start.1 = (bf16[88,1408]{1,0:T(8,128)(2,1)S(1)}, bf16[88,1408]{1,0:T(8,128)(2,1)}, u32[]{:S(2)}) copy-start(bf16[88,1408]{1,0:T(8,128)(2,1)} %param.5) | copy-start | bytes 743428
  13.7 10.3 %all-to-all-start.3 = ((bf16[88,4,352]{2,0,1:T(8,128)(2,1)}), bf16[88,4,352]{2,0,1:T(8,128)(2,1)}, u32[]{:S(2)}, u32[]{:S(2)}) async-start(bf16[88,4,352]{2,0,1:T(8,128)(2,1)} %copy.37), calls=%async_computation.3 | async-start | bytes 540672 | tf_op jit(solution)/shard_map/all_to_all | solution.py:34
  18.1 20.0 %copy-start.4 = (f32[1408]{0:T(1024)S(1)}, f32[1408]{0:T(1024)}, u32[]{:S(2)}) copy-start(f32[1408]{0:T(1024)} %param.9) | copy-start | bytes 16900
  24.0 10.2 %all-to-all-start.6 = ((bf16[88,4,352]{2,0,1:T(8,128)(2,1)}), bf16[88,4,352]{2,0,1:T(8,128)(2,1)}, u32[]{:S(2)}, u32[]{:S(2)}) async-start(bf16[88,4,352]{2,0,1:T(8,128)(2,1)} %copy.41), calls=%async_computation.6 | async-start | bytes 540672 | tf_op jit(solution)/shard_map/all_to_all | solution.py:35
  34.2 9.3 %all-to-all-start.1 = ((bf16[2,2,88,352]{3,2,1,0:T(8,128)(2,1)}), bf16[2,2,88,352]{3,2,1,0:T(8,128)(2,1)S(1)}, u32[]{:S(2)}, u32[]{:S(2)}) async-start(bf16[2,2,88,352]{3,2,1,0:T(8,128)(2,1)} %bitcast.1), calls=%async_computation.1 | async-start | bytes 540672 | tf_op jit(solution)/shard_map/all_to_all | solution.py:42
  43.5 8.7 %all-to-all-start.4 = ((bf16[2,2,88,352]{3,2,1,0:T(8,128)(2,1)}), bf16[2,2,88,352]{3,2,1,0:T(8,128)(2,1)S(1)}, u32[]{:S(2)}, u32[]{:S(2)}) async-start(bf16[2,2,88,352]{3,2,1,0:T(8,128)(2,1)} %bitcast.8), calls=%async_computation.4 | async-start | bytes 540672 | tf_op jit(solution)/shard_map/all_to_all | solution.py:42
  52.1 8.7 %all-to-all-start.7 = ((bf16[2,2,88,352]{3,2,1,0:T(8,128)(2,1)}), bf16[2,2,88,352]{3,2,1,0:T(8,128)(2,1)S(1)}, u32[]{:S(2)}, u32[]{:S(2)}) async-start(bf16[2,2,88,352]{3,2,1,0:T(8,128)(2,1)} %bitcast.15), calls=%async_computation.7 | async-start | bytes 540672 | tf_op jit(solution)/shard_map/all_to_all | solution.py:42
  60.8 53.9 %all-to-all-start.2 = ((bf16[4,1,1,88,352]{4,3,2,1,0:T(8,128)(2,1)}), bf16[4,1,1,88,352]{4,3,2,1,0:T(8,128)(2,1)S(1)}, u32[]{:S(2)}, u32[]{:S(2)}) async-start(bf16[4,1,1,88,352]{4,3,2,1,0:T(8,128)(2,1)} %bitcast.5), calls=%async_computation.2 | async-start | bytes 540672 | tf_op jit(solution)/shard_map/all_to_all | solution.py:50
  114.7 14.7 %all-to-all-start.5 = ((bf16[4,1,1,88,352]{4,3,2,1,0:T(8,128)(2,1)}), bf16[4,1,1,88,352]{4,3,2,1,0:T(8,128)(2,1)S(1)}, u32[]{:S(2)}, u32[]{:S(2)}) async-start(bf16[4,1,1,88,352]{4,3,2,1,0:T(8,128)(2,1)} %bitcast.12), calls=%async_computation.5 | async-start | bytes 540672 | tf_op jit(solution)/shard_map/all_to_all | solution.py:50
  129.4 17.4 %all-to-all-start.8 = ((bf16[4,1,1,88,352]{4,3,2,1,0:T(8,128)(2,1)}), bf16[4,1,1,88,352]{4,3,2,1,0:T(8,128)(2,1)S(1)}, u32[]{:S(2)}, u32[]{:S(2)}) async-start(bf16[4,1,1,88,352]{4,3,2,1,0:T(8,128)(2,1)} %bitcast.19), calls=%async_computation.8 | async-start | bytes 540672 | tf_op jit(solution)/shard_map/all_to_all | solution.py:50
